TPU v7x, 32 devices: a whole 2x2x4 slice. The times are simulated.
32 devices in a mesh: dom: 8 (over z, y), sub: 4 (over x, core).
Axes of the slice: x: 2, y: 2, z: 4, core: 2. Of those that a mesh axis runs over, the one named last changes fastest.
Arguments:
- positions: float32 [2048, 3, 256], P(('dom', 'sub')), may hold values from -6 to 6
- time_bins: int32 [2048, 256], P(('dom', 'sub')), may hold values from 0 to 5
- home_groups: int32 [2048], P(('dom', 'sub')), may hold values from 0 to 63
- targets: int32 [2048, 4], P(('dom', 'sub')), may hold values from -1 to 7, as said below
- target_groups: int32 [2048, 4], P(('dom', 'sub')), may hold values from 0 to 63
- node_pos: float32 [3, 131072], P(None, ('dom', 'sub')), may hold values from -6 to 6
- node_mass: float32 [131072], P(('dom', 'sub')), may hold values from 0.2 to 2
- node_lists: int32 [512, 256], P('dom'), may hold values from 0 to 16383
- list_counts: int32 [512], P('dom'), may hold values from 64 to 256, as said below
Outputs:
- forces: float32 [2048, 3, 256], P(('dom', 'sub'))
Inputs may be any that keep to these rules, and one draw needn't show every extreme that they name: `targets`: row b names the remote domains that block b visits, each at most once and never its own domain b // 256; -1 marks an unused entry, in any column. The rows of one device name one domain at most 32 times, and some device names some domain exactly 32 times in every draw. The rows of one domain's 4 devices together name one domain at most 64 times, and this is reached in every draw. `list_counts`: each domain has at least one list with all 256 entries valid.
All inputs are finite; a program needn't handle non-finite values.
Results may differ from a plain program's by a relative error of at most 0.0003.
Values sent between devices are 32-bit elements; how exact they have to be, the bound alone decides.
A program may use at most 128 MiB of HBM per device.

v0:
```python
import jax
import jax.numpy as jnp
from jax import lax
from jax.sharding import PartitionSpec as P

CUR_BIN = 2
soften_sq = 0.04
gauss_slope = 1.1283791670955126


def prefix(part, axis, combine, identity):
    place = lax.axis_index(axis)
    gathered = lax.all_gather(part, axis)
    state = jnp.zeros_like(part) + jnp.asarray(identity, part.dtype)

    def one(step, state):
        return combine(state, lax.dynamic_index_in_dim(gathered, step, 0, False))

    return lax.fori_loop(0, place, one, state)


def short_pull(sink_pos, source_pos, source_mass):
    offset = sink_pos[:, None, :] - source_pos[:, :, None]
    range_sq = jnp.sum(offset * offset, axis=0) + soften_sq
    distance = jnp.sqrt(range_sq)
    scaled = distance * 0.5
    factor = lax.erfc(scaled) + gauss_slope * scaled * jnp.exp(-scaled * scaled)
    weight = source_mass[:, None] * factor / (range_sq * distance)
    return -jnp.sum(offset * weight[None, :, :], axis=1)


def list_tables(table_pos, table_mass, lists, counts):
    entry_ids = jnp.arange(lists.shape[1], dtype=jnp.int32)
    list_pos = jnp.transpose(table_pos[:, lists], (1, 0, 2))
    list_mass = table_mass[lists] * (entry_ids[None, :] < counts[:, None]).astype(jnp.float32)
    return (list_pos, list_mass)


def evaluate(sink_pos, list_rows, is_alive, list_pos, list_mass):
    item_count = sink_pos.shape[0]
    padded = -(-item_count // 8) * 8

    def one_item(sink_one, list_row, alive_one):
        return short_pull(sink_one, list_pos[list_row], list_mass[list_row] * alive_one)

    def one_group(operands):
        return jax.vmap(one_item)(*operands)

    width = sink_pos.shape[2]
    grouped = lax.map(
        one_group,
        (
            sink_pos.reshape(padded // 8, 8, 3, width),
            list_rows.reshape(padded // 8, 8),
            is_alive.reshape(padded // 8, 8),
        ),
    )
    return grouped.reshape(padded, 3, width)[:item_count]


def ranks_within(bucket, usable, bucket_count):
    onehot = (
        (bucket[:, None] == jnp.arange(bucket_count, dtype=jnp.int32)[None, :]) & usable[:, None]
    ).astype(jnp.int32)
    placed = jnp.sum((jnp.cumsum(onehot, axis=0) - onehot) * onehot, axis=1)
    return (placed, jnp.sum(onehot, axis=0))


def owners(slot_index, usable, slot_count):
    matches = (slot_index[None, :] == jnp.arange(slot_count, dtype=jnp.int32)[:, None]) & usable[
        None, :
    ]
    is_filled = jnp.any(matches, axis=1)
    source_row = jnp.sum(
        matches.astype(jnp.int32) * jnp.arange(slot_index.shape[0], dtype=jnp.int32)[None, :],
        axis=1,
    )
    return (source_row, is_filled)


def local(
    positions,
    time_bins,
    home_groups,
    targets,
    target_groups,
    node_pos,
    node_mass,
    node_lists,
    list_counts,
):
    domains = lax.axis_size("dom")
    sharers = lax.axis_size("sub")
    blocks, most_visits = targets.shape
    width = positions.shape[2]
    capacity = max(2, blocks * most_visits // domains)
    table_pos, table_mass = (
        lax.all_gather(node_pos, "sub", axis=1, tiled=True),
        lax.all_gather(node_mass, "sub", axis=0, tiled=True),
    )
    list_pos, list_mass = list_tables(table_pos, table_mass, node_lists, list_counts)
    home_force = evaluate(
        positions, home_groups, jnp.ones((blocks,), jnp.float32), list_pos, list_mass
    )
    flat_dest = targets.reshape(-1)
    usable = flat_dest >= 0
    safe_dest = jnp.maximum(flat_dest, 0)
    pair_block = jnp.arange(blocks * most_visits, dtype=jnp.int32) // most_visits
    flat_groups = target_groups.reshape(-1)
    within, per_domain = ranks_within(safe_dest, usable, domains)
    first_width = -(-capacity // sharers)
    second_width = -(-2 * capacity // sharers)
    offsets = prefix(
        per_domain, "sub", lambda earlier, later: earlier + later, jnp.zeros_like(per_domain)
    )
    row_place = offsets[safe_dest] + within
    sharer_of = row_place % sharers
    row_slot = row_place // sharers
    bucket = sharer_of * domains + safe_dest
    within_bucket, _ = ranks_within(bucket, usable, sharers * domains)
    first_slot = bucket * first_width + within_bucket
    source_row, is_filled = owners(first_slot, usable, sharers * domains * first_width)
    out_pos = jnp.where(is_filled[:, None, None], positions[pair_block[source_row]], 0.0).reshape(
        sharers, domains, first_width, 3, width
    )
    out_group = jnp.where(is_filled, flat_groups[source_row], -1).reshape(
        sharers, domains, first_width
    )
    out_slot = jnp.where(is_filled, row_slot[source_row], 0).reshape(sharers, domains, first_width)
    spread_pos, spread_group, spread_slot = (
        lax.all_to_all(out_pos, "sub", split_axis=0, concat_axis=0, tiled=True),
        lax.all_to_all(out_group, "sub", split_axis=0, concat_axis=0, tiled=True),
        lax.all_to_all(out_slot, "sub", split_axis=0, concat_axis=0, tiled=True),
    )
    arrival_dest = (
        jnp.arange(sharers * domains * first_width, dtype=jnp.int32) // first_width % domains
    )
    arrival_group = spread_group.reshape(-1)
    arrival_ok = arrival_group >= 0
    second_index = arrival_dest * second_width + spread_slot.reshape(-1)
    arrival_row, second_filled = owners(second_index, arrival_ok, domains * second_width)
    mid_pos = jnp.where(
        second_filled[:, None, None], spread_pos.reshape(-1, 3, width)[arrival_row], 0.0
    ).reshape(domains, second_width, 3, width)
    mid_group = jnp.where(second_filled, arrival_group[arrival_row], -1).reshape(
        domains, second_width
    )
    arrived_pos = lax.all_to_all(mid_pos, "dom", split_axis=0, concat_axis=0, tiled=True)
    arrived_group = lax.all_to_all(mid_group, "dom", split_axis=0, concat_axis=0, tiled=True)
    leading = arrived_group.shape
    flat_group = arrived_group.reshape(-1)
    pulled = evaluate(
        arrived_pos.reshape((-1, 3, width)),
        jnp.maximum(flat_group, 0),
        (flat_group >= 0).astype(jnp.float32),
        list_pos,
        list_mass,
    )
    computed = pulled.reshape(leading + (3, width))
    returned = lax.all_to_all(computed, "dom", split_axis=0, concat_axis=0, tiled=True)
    arrival_force = returned.reshape(domains * second_width, 3, width)[
        jnp.where(arrival_ok, second_index, 0)
    ]
    arrival_force = arrival_force * arrival_ok.astype(jnp.float32)[:, None, None]
    gathered_back = lax.all_to_all(
        arrival_force.reshape(sharers, domains, first_width, 3, width),
        "sub",
        split_axis=0,
        concat_axis=0,
        tiled=True,
    )
    pair_force = gathered_back.reshape(-1, 3, width)[jnp.where(usable, first_slot, 0)]
    pair_force = pair_force * usable.astype(jnp.float32)[:, None, None]
    remote = jnp.sum(pair_force.reshape(blocks, most_visits, 3, width), axis=1)
    active = (time_bins <= CUR_BIN).astype(jnp.float32)
    return (home_force + remote) * active[:, None, :]


def solution(mesh):
    return jax.shard_map(
        local,
        mesh=mesh,
        in_specs=(
            P(("dom", "sub"), None, None),
            P(("dom", "sub"), None),
            P(("dom", "sub")),
            P(("dom", "sub"), None),
            P(("dom", "sub"), None),
            P(None, ("dom", "sub")),
            P(("dom", "sub")),
            P("dom", None),
            P("dom"),
        ),
        out_specs=P(("dom", "sub"), None, None),
        check_vma=False,
    )
```

profile of v0, /device:TPU:0, one launch (start us, length us, event | category | flops | bytes accessed | tf_op | source)
XLA Modules:
  0.0 551.8 jit_solution(571146538005920362)
XLA Ops:
  2.9 1.3 dynamic-slice
  5.3 6.4 %all-reduce.4 = s32[32]{0:T(128)S(1)} all-reduce(s32[32]{0:T(128)S(1)} %dynamic-update-slice), channel_id=2, replica_groups=mesh['dom'=8,'sub'=4] {'sub'}, use_global_device_ids=true, to_apply=%add.4 | all-reduce | flops 32 | bytes 256
  12.5 5.0 and_select_fusion.4
  18.7 1.9 gather_fusion.6
  21.6 1.9 gather_fusion.7
  24.4 3.2 all-to-all-start
  27.7 1.9 gather_fusion.8
  29.7 1.9 gather_fusion.9
  32.7 3.3 all-to-all-start.1
  36.0 3.7 all-to-all-done.1
  39.8 3.5 all-to-all-start.2
  43.5 1.3 gather_fusion.11
  45.7 9.2 %all-to-all-done.2 = f32[4,8,8,3,256]{4,2,1,3,0:T(8,128)S(1)} async-done(((f32[4,8,8,3,256]{4,2,1,3,0:T(8,128)}), f32[4,8,8,3,256]{4,2,1,3,0:T(8,128)S(1)}, u32[]{:S(2)}, u32[]{:S(2)}) %all-to-all-start.2) | async-done | bytes 786464 | tf_op jit(solution)/shard_map/all_to_all | solution.py:131
  54.9 5.8 %all-to-all-start.4 = ((s32[8,1,16]{2,1,0:T(1,128)}), s32[8,1,16]{2,1,0:T(1,128)S(1)}, u32[]{:S(2)}, u32[]{:S(2)}) async-start(s32[8,1,16]{2,1,0:T(1,128)} %bitcast.37), calls=%async_computation.4 | async-start | bytes 8192 | tf_op jit(solution)/shard_map/all_to_all | solution.py:149
  63.0 4.1 all-to-all-done.4
  67.1 3.5 all-to-all-start.3
  71.3 49.3 %all_gather.12 = f32[3,16384]{0,1:T(8,128)} all-gather(f32[3,4096]{0,1:T(8,128)S(1)} %copy.99), channel_id=1, replica_groups=mesh['dom'=8,'sub'=4] {'sub'}, dimensions={1}, use_global_device_ids=true | all-gather | bytes 245760 | tf_op jit(solution)/shard_map/all_gather | solution.py:98
  120.6 57.8 %gather_fusion.4 = f32[16384,3]{1,0:T(8,128)} fusion(f32[3,16384]{0,1:T(8,128)} %all_gather.12, s32[16384]{0:T(1024)S(1)} %broadcast_clamp_fusion), kind=kCustom, calls=%fused_computation.4 | custom fusion | bytes 458752 | tf_op jit(solution)/shard_map/gather | solution.py:34
  178.4 5.4 copy.100
  183.7 5.2 all_gather.13
  189.0 90.5 %gather_fusion.5 = f32[16384]{0:T(1024)S(1)} fusion(f32[16384]{0:T(1024)S(1)} %all_gather.13, s32[16384]{0:T(1024)S(1)} %broadcast_clamp_fusion), kind=kCustom, calls=%fused_computation.5 | custom fusion | bytes 196608 | tf_op jit(solution)/shard_map/gather | solution.py:35
  279.8 160.7 %while.36 = (s32[]{:T(128)}, f32[16,8,3,256]{3,2,1,0:T(4,128)}, f32[16,8,3,256]{3,1,0,2:T(8,128)S(1)}, s32[16,8]{1,0:T(8,128)S(1)}, f32[64,3,256]{2,1,0:T(4,128)...) while((s32[]{:T(128)}, f32[16,8,3,256]{3,2,1,0:T(4,128)}, ...), condition=%wide.region_20.21_spmd, body=%wide.region_17.20_spmd.sunk | while | flops 45615144 | bytes 8758177 | solution.py:50
  280.5 1.1 fusion.88
  282.3 5.9 %fusion.90 = f32[8,256,256]{2,1,0:T(8,128)S(1)} fusion(f32[8,256,256]{2,1,0:T(8,128)S(1)} %fusion.88, f32[8,256]{1,0:T(8,128)S(1)} %broadcast_multiply_fusion.3), kind=kLoop, calls=%fused_computation.57.clone.1 | loop fusion | flops 36700160 | bytes 4202496 | tf_op jit(solution)/shard_map/while/body/eval_jaxpr/vmap()/div | solution.py:28
  290.6 1.1 fusion.88
  292.4 5.9 %fusion.90 = f32[8,256,256]{2,1,0:T(8,128)S(1)} fusion(f32[8,256,256]{2,1,0:T(8,128)S(1)} %fusion.88, f32[8,256]{1,0:T(8,128)S(1)} %broadcast_multiply_fusion.3), kind=kLoop, calls=%fused_computation.57.clone.1 | loop fusion | flops 36700160 | bytes 4202496 | tf_op jit(solution)/shard_map/while/body/eval_jaxpr/vmap()/div | solution.py:28
  300.6 1.1 fusion.88
  302.4 5.9 %fusion.90 = f32[8,256,256]{2,1,0:T(8,128)S(1)} fusion(f32[8,256,256]{2,1,0:T(8,128)S(1)} %fusion.88, f32[8,256]{1,0:T(8,128)S(1)} %broadcast_multiply_fusion.3), kind=kLoop, calls=%fused_computation.57.clone.1 | loop fusion | flops 36700160 | bytes 4202496 | tf_op jit(solution)/shard_map/while/body/eval_jaxpr/vmap()/div | solution.py:28
  310.6 1.1 fusion.88
  312.4 5.9 %fusion.90 = f32[8,256,256]{2,1,0:T(8,128)S(1)} fusion(f32[8,256,256]{2,1,0:T(8,128)S(1)} %fusion.88, f32[8,256]{1,0:T(8,128)S(1)} %broadcast_multiply_fusion.3), kind=kLoop, calls=%fused_computation.57.clone.1 | loop fusion | flops 36700160 | bytes 4202496 | tf_op jit(solution)/shard_map/while/body/eval_jaxpr/vmap()/div | solution.py:28
  320.7 1.1 fusion.88
  322.5 5.9 %fusion.90 = f32[8,256,256]{2,1,0:T(8,128)S(1)} fusion(f32[8,256,256]{2,1,0:T(8,128)S(1)} %fusion.88, f32[8,256]{1,0:T(8,128)S(1)} %broadcast_multiply_fusion.3), kind=kLoop, calls=%fused_computation.57.clone.1 | loop fusion | flops 36700160 | bytes 4202496 | tf_op jit(solution)/shard_map/while/body/eval_jaxpr/vmap()/div | solution.py:28
  330.7 1.1 fusion.88
  332.5 5.9 %fusion.90 = f32[8,256,256]{2,1,0:T(8,128)S(1)} fusion(f32[8,256,256]{2,1,0:T(8,128)S(1)} %fusion.88, f32[8,256]{1,0:T(8,128)S(1)} %broadcast_multiply_fusion.3), kind=kLoop, calls=%fused_computation.57.clone.1 | loop fusion | flops 36700160 | bytes 4202496 | tf_op jit(solution)/shard_map/while/body/eval_jaxpr/vmap()/div | solution.py:28
  340.8 1.1 fusion.88
  342.6 5.9 %fusion.90 = f32[8,256,256]{2,1,0:T(8,128)S(1)} fusion(f32[8,256,256]{2,1,0:T(8,128)S(1)} %fusion.88, f32[8,256]{1,0:T(8,128)S(1)} %broadcast_multiply_fusion.3), kind=kLoop, calls=%fused_computation.57.clone.1 | loop fusion | flops 36700160 | bytes 4202496 | tf_op jit(solution)/shard_map/while/body/eval_jaxpr/vmap()/div | solution.py:28
  350.8 1.1 fusion.88
  352.6 5.9 %fusion.90 = f32[8,256,256]{2,1,0:T(8,128)S(1)} fusion(f32[8,256,256]{2,1,0:T(8,128)S(1)} %fusion.88, f32[8,256]{1,0:T(8,128)S(1)} %broadcast_multiply_fusion.3), kind=kLoop, calls=%fused_computation.57.clone.1 | loop fusion | flops 36700160 | bytes 4202496 | tf_op jit(solution)/shard_map/while/body/eval_jaxpr/vmap()/div | solution.py:28
  360.9 1.1 fusion.88
  362.6 5.9 %fusion.90 = f32[8,256,256]{2,1,0:T(8,128)S(1)} fusion(f32[8,256,256]{2,1,0:T(8,128)S(1)} %fusion.88, f32[8,256]{1,0:T(8,128)S(1)} %broadcast_multiply_fusion.3), kind=kLoop, calls=%fused_computation.57.clone.1 | loop fusion | flops 36700160 | bytes 4202496 | tf_op jit(solution)/shard_map/while/body/eval_jaxpr/vmap()/div | solution.py:28
  370.9 1.1 fusion.88
  372.7 5.9 %fusion.90 = f32[8,256,256]{2,1,0:T(8,128)S(1)} fusion(f32[8,256,256]{2,1,0:T(8,128)S(1)} %fusion.88, f32[8,256]{1,0:T(8,128)S(1)} %broadcast_multiply_fusion.3), kind=kLoop, calls=%fused_computation.57.clone.1 | loop fusion | flops 36700160 | bytes 4202496 | tf_op jit(solution)/shard_map/while/body/eval_jaxpr/vmap()/div | solution.py:28
  380.9 1.1 fusion.88
  382.7 5.9 %fusion.90 = f32[8,256,256]{2,1,0:T(8,128)S(1)} fusion(f32[8,256,256]{2,1,0:T(8,128)S(1)} %fusion.88, f32[8,256]{1,0:T(8,128)S(1)} %broadcast_multiply_fusion.3), kind=kLoop, calls=%fused_computation.57.clone.1 | loop fusion | flops 36700160 | bytes 4202496 | tf_op jit(solution)/shard_map/while/body/eval_jaxpr/vmap()/div | solution.py:28
  392.8 5.9 %fusion.90 = f32[8,256,256]{2,1,0:T(8,128)S(1)} fusion(f32[8,256,256]{2,1,0:T(8,128)S(1)} %fusion.88, f32[8,256]{1,0:T(8,128)S(1)} %broadcast_multiply_fusion.3), kind=kLoop, calls=%fused_computation.57.clone.1 | loop fusion | flops 36700160 | bytes 4202496 | tf_op jit(solution)/shard_map/while/body/eval_jaxpr/vmap()/div | solution.py:28
  402.8 5.9 %fusion.90 = f32[8,256,256]{2,1,0:T(8,128)S(1)} fusion(f32[8,256,256]{2,1,0:T(8,128)S(1)} %fusion.88, f32[8,256]{1,0:T(8,128)S(1)} %broadcast_multiply_fusion.3), kind=kLoop, calls=%fused_computation.57.clone.1 | loop fusion | flops 36700160 | bytes 4202496 | tf_op jit(solution)/shard_map/while/body/eval_jaxpr/vmap()/div | solution.py:28
  412.9 5.9 %fusion.90 = f32[8,256,256]{2,1,0:T(8,128)S(1)} fusion(f32[8,256,256]{2,1,0:T(8,128)S(1)} %fusion.88, f32[8,256]{1,0:T(8,128)S(1)} %broadcast_multiply_fusion.3), kind=kLoop, calls=%fused_computation.57.clone.1 | loop fusion | flops 36700160 | bytes 4202496 | tf_op jit(solution)/shard_map/while/body/eval_jaxpr/vmap()/div | solution.py:28
  422.9 5.9 %fusion.90 = f32[8,256,256]{2,1,0:T(8,128)S(1)} fusion(f32[8,256,256]{2,1,0:T(8,128)S(1)} %fusion.88, f32[8,256]{1,0:T(8,128)S(1)} %broadcast_multiply_fusion.3), kind=kLoop, calls=%fused_computation.57.clone.1 | loop fusion | flops 36700160 | bytes 4202496 | tf_op jit(solution)/shard_map/while/body/eval_jaxpr/vmap()/div | solution.py:28
  432.9 5.9 %fusion.90 = f32[8,256,256]{2,1,0:T(8,128)S(1)} fusion(f32[8,256,256]{2,1,0:T(8,128)S(1)} %fusion.88, f32[8,256]{1,0:T(8,128)S(1)} %broadcast_multiply_fusion.3), kind=kLoop, calls=%fused_computation.57.clone.1 | loop fusion | flops 36700160 | bytes 4202496 | tf_op jit(solution)/shard_map/while/body/eval_jaxpr/vmap()/div | solution.py:28
  440.5 1.9 copy.114
  442.4 5.9 %all-to-all-start.5 = ((f32[8,16,3,256]{3,1,2,0:T(8,128)}), f32[8,16,3,256]{3,1,2,0:T(8,128)S(1)}, u32[]{:S(2)}, u32[]{:S(2)}) async-start(f32[8,16,3,256]{3,1,2,0:T(8,128)} %copy.114), calls=%async_computation.5 | async-start | bytes 786432 | tf_op jit(solution)/shard_map/all_to_all | solution.py:160
  448.8 11.7 %all-to-all-done.5 = f32[8,16,3,256]{3,1,2,0:T(8,128)S(1)} async-done(((f32[8,16,3,256]{3,1,2,0:T(8,128)}), f32[8,16,3,256]{3,1,2,0:T(8,128)S(1)}, u32[]{:S(2)}, u32[]{:S(2)}) %all-to-all-start.5) | async-done | bytes 393248 | tf_op jit(solution)/shard_map/all_to_all | solution.py:160
  460.8 1.3 gather_fusion.12
  463.3 3.5 all-to-all-start.6
  466.8 80.5 %while.34 = (s32[]{:T(128)}, f32[8,8,3,256]{3,2,1,0:T(4,128)}, f32[8,8,3,256]{3,2,1,0:T(4,128)S(1)}, s32[8,8]{1,0:T(8,128)S(1)}, f32[64,3,256]{2,1,0:T(4,128)S(1)}, /*index=5*/f32[64,256]{1,0:T(8,128)S(1)}, s32[]{:T(128)}) while((s32[]{:T(128)}, f32[8,8,3,256]{3,2,1,0:T(4,128)}, f32[8,8,3,256]{3,2,1,0:T(4,128)S(1)}, s32[8,8]{1,0:T(8,128)S(1)}, ...), condition=%wide.region_3.4_spmd, body=%wide.region_0.3_spmd.sunk | while | flops 45613096 | bytes 10265453 | solution.py:50
  469.3 5.9 %fusion.86 = f32[8,256,256]{2,1,0:T(8,128)S(1)} fusion(f32[8,256,256]{2,1,0:T(8,128)S(1)} %fusion.85, f32[8,256]{1,0:T(8,128)S(1)} %gather_fusion.1), kind=kLoop, calls=%fused_computation.27.clone.1 | loop fusion | flops 36700160 | bytes 4202496 | tf_op jit(solution)/shard_map/while/body/eval_jaxpr/vmap()/div | solution.py:28
  479.3 5.9 %fusion.86 = f32[8,256,256]{2,1,0:T(8,128)S(1)} fusion(f32[8,256,256]{2,1,0:T(8,128)S(1)} %fusion.85, f32[8,256]{1,0:T(8,128)S(1)} %gather_fusion.1), kind=kLoop, calls=%fused_computation.27.clone.1 | loop fusion | flops 36700160 | bytes 4202496 | tf_op jit(solution)/shard_map/while/body/eval_jaxpr/vmap()/div | solution.py:28
  489.4 5.9 %fusion.86 = f32[8,256,256]{2,1,0:T(8,128)S(1)} fusion(f32[8,256,256]{2,1,0:T(8,128)S(1)} %fusion.85, f32[8,256]{1,0:T(8,128)S(1)} %gather_fusion.1), kind=kLoop, calls=%fused_computation.27.clone.1 | loop fusion | flops 36700160 | bytes 4202496 | tf_op jit(solution)/shard_map/while/body/eval_jaxpr/vmap()/div | solution.py:28
  499.4 5.9 %fusion.86 = f32[8,256,256]{2,1,0:T(8,128)S(1)} fusion(f32[8,256,256]{2,1,0:T(8,128)S(1)} %fusion.85, f32[8,256]{1,0:T(8,128)S(1)} %gather_fusion.1), kind=kLoop, calls=%fused_computation.27.clone.1 | loop fusion | flops 36700160 | bytes 4202496 | tf_op jit(solution)/shard_map/while/body/eval_jaxpr/vmap()/div | solution.py:28
  509.5 5.9 %fusion.86 = f32[8,256,256]{2,1,0:T(8,128)S(1)} fusion(f32[8,256,256]{2,1,0:T(8,128)S(1)} %fusion.85, f32[8,256]{1,0:T(8,128)S(1)} %gather_fusion.1), kind=kLoop, calls=%fused_computation.27.clone.1 | loop fusion | flops 36700160 | bytes 4202496 | tf_op jit(solution)/shard_map/while/body/eval_jaxpr/vmap()/div | solution.py:28
  519.5 5.9 %fusion.86 = f32[8,256,256]{2,1,0:T(8,128)S(1)} fusion(f32[8,256,256]{2,1,0:T(8,128)S(1)} %fusion.85, f32[8,256]{1,0:T(8,128)S(1)} %gather_fusion.1), kind=kLoop, calls=%fused_computation.27.clone.1 | loop fusion | flops 36700160 | bytes 4202496 | tf_op jit(solution)/shard_map/while/body/eval_jaxpr/vmap()/div | solution.py:28
  529.6 5.9 %fusion.86 = f32[8,256,256]{2,1,0:T(8,128)S(1)} fusion(f32[8,256,256]{2,1,0:T(8,128)S(1)} %fusion.85, f32[8,256]{1,0:T(8,128)S(1)} %gather_fusion.1), kind=kLoop, calls=%fused_computation.27.clone.1 | loop fusion | flops 36700160 | bytes 4202496 | tf_op jit(solution)/shard_map/while/body/eval_jaxpr/vmap()/div | solution.py:28
  539.7 5.9 %fusion.86 = f32[8,256,256]{2,1,0:T(8,128)S(1)} fusion(f32[8,256,256]{2,1,0:T(8,128)S(1)} %fusion.85, f32[8,256]{1,0:T(8,128)S(1)} %gather_fusion.1), kind=kLoop, calls=%fused_computation.27.clone.1 | loop fusion | flops 36700160 | bytes 4202496 | tf_op jit(solution)/shard_map/while/body/eval_jaxpr/vmap()/div | solution.py:28
  548.3 1.3 gather_fusion.13
  (347 shorter events, 104.2 us)
Async XLA Ops:
  0.0 29.6 %copy-start = (f32[64,3,256]{2,0,1:T(8,128)S(1)}, f32[64,3,256]{2,0,1:T(8,128)}, u32[]{:S(2)}) copy-start(f32[64,3,256]{2,0,1:T(8,128)} %param.15) | copy-start | bytes 589828
  24.4 8.3 %all-to-all-start = ((s32[4,8,8]{2,1,0:T(8,128)}), s32[4,8,8]{2,1,0:T(8,128)S(1)}, u32[]{:S(2)}, u32[]{:S(2)}) async-start(s32[4,8,8]{2,1,0:T(8,128)} %get-tuple-element.261), calls=%async_computation | async-start | bytes 32768 | tf_op jit(solution)/shard_map/all_to_all | solution.py:133
  29.6 3.0 copy-start.4
  32.7 7.1 %all-to-all-start.1 = ((s32[4,8,8]{2,1,0:T(8,128)}), s32[4,8,8]{2,1,0:T(8,128)S(1)}, u32[]{:S(2)}, u32[]{:S(2)}) async-start(s32[4,8,8]{2,1,0:T(8,128)} %get-tuple-element.260), calls=%async_computation.1 | async-start | bytes 32768 | tf_op jit(solution)/shard_map/all_to_all | solution.py:132
  39.8 15.1 %all-to-all-start.2 = ((f32[4,8,8,3,256]{4,2,1,3,0:T(8,128)}), f32[4,8,8,3,256]{4,2,1,3,0:T(8,128)S(1)}, u32[]{:S(2)}, u32[]{:S(2)}) async-start(f32[4,8,8,3,256]{4,2,1,3,0:T(8,128)} %copy_select_fusion), calls=%async_computation.2 | async-start | bytes 1572864 | tf_op jit(solution)/shard_map/all_to_all | solution.py:131
  54.9 12.3 %all-to-all-start.4 = ((s32[8,1,16]{2,1,0:T(1,128)}), s32[8,1,16]{2,1,0:T(1,128)S(1)}, u32[]{:S(2)}, u32[]{:S(2)}) async-start(s32[8,1,16]{2,1,0:T(1,128)} %bitcast.37), calls=%async_computation.4 | async-start | bytes 8192 | tf_op jit(solution)/shard_map/all_to_all | solution.py:149
  60.7 9.9 %copy-start.3 = (f32[3,4096]{1,0:T(4,128)S(1)}, f32[3,4096]{1,0:T(4,128)}, u32[]{:S(2)}) copy-start(f32[3,4096]{1,0:T(4,128)} %param.20) | copy-start | bytes 147460
  67.1 212.7 %all-to-all-start.3 = ((f32[8,16,3,256]{3,1,2,0:T(8,128)}), f32[8,16,3,256]{3,1,2,0:T(8,128)S(1)}, u32[]{:S(2)}, u32[]{:S(2)}) async-start(f32[8,16,3,256]{3,1,2,0:T(8,128)} %copy_select_fusion.1), calls=%async_computation.3 | async-start | bytes 786432 | tf_op jit(solution)/shard_map/all_to_all | solution.py:148
  178.4 5.4 copy-start.6
  189.0 90.6 %copy-start.7 = (s32[64]{0:T(128)S(1)}, s32[64]{0:T(128)}, u32[]{:S(2)}) copy-start(s32[64]{0:T(128)} %param.23) | copy-start | bytes 772
  440.5 7.9 %copy-start.8 = (s32[64]{0:T(128)S(1)}, s32[64]{0:T(128)}, u32[]{:S(2)}) copy-start(s32[64]{0:T(128)} %param.17) | copy-start | bytes 772
  442.4 18.1 %all-to-all-start.5 = ((f32[8,16,3,256]{3,1,2,0:T(8,128)}), f32[8,16,3,256]{3,1,2,0:T(8,128)S(1)}, u32[]{:S(2)}, u32[]{:S(2)}) async-start(f32[8,16,3,256]{3,1,2,0:T(8,128)} %copy.114), calls=%async_computation.5 | async-start | bytes 786432 | tf_op jit(solution)/shard_map/all_to_all | solution.py:160
  463.3 84.4 %all-to-all-start.6 = ((f32[4,8,8,3,256]{4,2,3,1,0:T(8,128)}), f32[4,8,8,3,256]{4,2,3,1,0:T(8,128)S(1)}, u32[]{:S(2)}, u32[]{:S(2)}) async-start(f32[4,8,8,3,256]{4,2,3,1,0:T(8,128)} %copy.118), calls=%async_computation.6 | async-start | bytes 1572864 | tf_op jit(solution)/shard_map/all_to_all | solution.py:165
  466.8 80.8 %copy-start.5 = (s32[64,256]{1,0:T(8,128)S(1)}, s32[64,256]{1,0:T(8,128)}, u32[]{:S(2)}) copy-start(s32[64,256]{1,0:T(8,128)} %param.16) | copy-start | bytes 196612
  466.8 0.7 copy-start.1
  475.2 1.7 copy-start.2
  476.9 0.7 copy-start.1
  485.2 1.7 copy-start.2
  486.9 0.7 copy-start.1
  495.3 1.7 copy-start.2
  497.0 0.7 copy-start.1
  505.3 1.7 copy-start.2
  507.1 0.7 copy-start.1
  515.4 1.7 copy-start.2
  517.1 0.7 copy-start.1
  525.4 1.7 copy-start.2
  527.2 0.7 copy-start.1
  535.5 1.7 copy-start.2
  537.2 0.7 copy-start.1
  545.6 1.7 copy-start.2
where the time goes:
time: 553 us; the launch traced here: 552 us
  other arithmetic  223 us (40%)
  local copies, waits for them, and re-layouts  208 us (38%)
  blocking collectives  60.9 us (11%)
  starting transfers between devices  28.7 us (5%)
  waiting for transfers between devices  28.7 us (5%)
    div x24, other arithmetic, short_pull(): weight = source_mass[:, None] * factor / (range_sq * distance)  141 us
    gather x2, local copies, waits for them, and re-layouts, list_tables(): table_mass[lists]  90.5 us
    gather x2, local copies, waits for them, and re-layouts, list_tables(): list_pos = jnp.transpose(table_pos[:, lists], (1, 0, 2))  63.1 us
    all_gather x1, blocking collectives, local(): lax.all_gather(node_pos, 'sub', axis=1, tiled=True)  49.3 us
    reduce_sum x24, other arithmetic, short_pull(): range_sq = jnp.sum(offset * offset, axis=0) + soften_sq  26.5 us
    reduce_sum x24, other arithmetic, short_pull(): return -jnp.sum(offset * weight[None, :, :], axis=1)  26.1 us
    dynamic_update_slice x24, other arithmetic, evaluate(): lax.map(one_group, (sink_pos.reshape(padded // 8, 8, 3, width), list_rows...  14.8 us
    gather x24, local copies, waits for them, and re-layouts, one_item(): list_pos[list_row]  14.4 us
  transfers between devices with their start and end apart: 7, of which 4 were waited for; matrix products, arithmetic and copies ran while one was open for 44% of the time, Pallas kernels for 0%

commit v1 on v0

--- a/solution.py
+++ b/solution.py
@@ -6,6 +6,9 @@
 CUR_BIN = 2
 soften_sq = 0.04
 gauss_slope = 1.1283791670955126
+lots_all_follow = lambda s0, mesh_name, out_dim: jnp.concatenate(
+    lax.all_gather(s0, axis_name=mesh_name), axis=out_dim
+)
 
 
 def prefix(part, axis, combine, identity):
@@ -95,7 +98,7 @@
     width = positions.shape[2]
     capacity = max(2, blocks * most_visits // domains)
     table_pos, table_mass = (
-        lax.all_gather(node_pos, "sub", axis=1, tiled=True),
+        lots_all_follow(node_pos, "sub", 1),
         lax.all_gather(node_mass, "sub", axis=0, tiled=True),
     )
     list_pos, list_mass = list_tables(table_pos, table_mass, node_lists, list_counts)

time: 553 us -> 513 us (0.928)
  blocking collectives: 60.9 us -> 17.6 us
    all_gather x1, blocking collectives: 49.3 us -> 5.78 us  [lax.all_gather(s0, axis_name=mesh_name)]
  transfers between devices with their start and end apart: 7 -> 7, of which waited for: 4 -> 4; matrix products, arithmetic and copies ran while one was open for 44% -> 48% of each run, Pallas kernels for 0% -> 0%
where the time goes in v1:
time: 513 us
  other arithmetic  223 us (43%)
  local copies, waits for them, and re-layouts  212 us (41%)
  starting transfers between devices  28.7 us (6%)
  waiting for transfers between devices  28.7 us (6%)
  blocking collectives  17.6 us (3%)
    div x24, other arithmetic, short_pull(): weight = source_mass[:, None] * factor / (range_sq * distance)  141 us
    gather x2, local copies, waits for them, and re-layouts, list_tables(): table_mass[lists]  90.5 us
    gather x2, local copies, waits for them, and re-layouts, list_tables(): list_pos = jnp.transpose(table_pos[:, lists], (1, 0, 2))  63.1 us
    reduce_sum x24, other arithmetic, short_pull(): range_sq = jnp.sum(offset * offset, axis=0) + soften_sq  26.5 us
    reduce_sum x24, other arithmetic, short_pull(): return -jnp.sum(offset * weight[None, :, :], axis=1)  26.1 us
    dynamic_update_slice x24, other arithmetic, evaluate(): lax.map(one_group, (sink_pos.reshape(padded // 8, 8, 3, width), list_rows...  14.8 us
    gather x24, local copies, waits for them, and re-layouts, one_item(): list_pos[list_row]  14.4 us
    gather x24, local copies, waits for them, and re-layouts, one_item(): list_mass[list_row] * alive_one  14 us
  transfers between devices with their start and end apart: 7, of which 4 were waited for; matrix products, arithmetic and copies ran while one was open for 48% of the time, Pallas kernels for 0%

profile of v1, /device:TPU:0, one launch (start us, length us, event | category | flops | bytes accessed | tf_op | source)
XLA Modules:
  0.0 512.6 jit_solution(11440188210197270234)
XLA Ops:
  2.9 1.3 dynamic-slice
  5.3 6.4 %all-reduce.4 = s32[32]{0:T(128)S(1)} all-reduce(s32[32]{0:T(128)S(1)} %dynamic-update-slice), channel_id=3, replica_groups=mesh['dom'=8,'sub'=4] {'sub'}, use_global_device_ids=true, to_apply=%add.4 | all-reduce | flops 32 | bytes 256
  12.5 5.0 and_select_fusion.4
  18.7 1.9 gather_fusion.6
  21.6 1.9 gather_fusion.7
  24.4 3.2 all-to-all-start
  27.7 1.9 gather_fusion.8
  29.7 1.9 gather_fusion.9
  32.7 3.3 all-to-all-start.1
  36.0 3.7 all-to-all-done.1
  39.8 3.5 all-to-all-start.2
  43.5 1.3 gather_fusion.11
  45.7 9.2 %all-to-all-done.2 = f32[4,8,8,3,256]{4,2,1,3,0:T(8,128)S(1)} async-done(((f32[4,8,8,3,256]{4,2,1,3,0:T(8,128)}), f32[4,8,8,3,256]{4,2,1,3,0:T(8,128)S(1)}, u32[]{:S(2)}, u32[]{:S(2)}) %all-to-all-start.2) | async-done | bytes 786464 | tf_op jit(solution)/shard_map/all_to_all | solution.py:134
  54.9 5.8 %all-to-all-start.4 = ((s32[8,1,16]{2,1,0:T(1,128)}), s32[8,1,16]{2,1,0:T(1,128)S(1)}, u32[]{:S(2)}, u32[]{:S(2)}) async-start(s32[8,1,16]{2,1,0:T(1,128)} %bitcast.40), calls=%async_computation.4 | async-start | bytes 8192 | tf_op jit(solution)/shard_map/all_to_all | solution.py:152
  63.0 4.1 all-to-all-done.4
  67.1 3.5 all-to-all-start.3
  70.6 5.8 %all-gather.2 = f32[4,3,4096]{2,1,0:T(4,128)S(1)} all-gather(f32[1,3,4096]{2,1,0:T(4,128)S(1)} %bitcast.134), channel_id=2, replica_groups=mesh['dom'=8,'sub'=4] {'sub'}, dimensions={0}, use_global_device_ids=true | all-gather | bytes 245760 | tf_op jit(solution)/shard_map/all_gather | solution.py:10
  76.4 4.8 copy.99
  81.2 57.8 %gather_fusion.4 = f32[16384,3]{1,0:T(8,128)} fusion(f32[3,16384]{0,1:T(8,128)} %bitcast.119, s32[16384]{0:T(1024)S(1)} %broadcast_clamp_fusion), kind=kCustom, calls=%fused_computation.4 | custom fusion | bytes 458752 | tf_op jit(solution)/shard_map/gather | solution.py:37
  139.0 5.4 %copy.100 = f32[64,256,3]{1,2,0:T(4,128)S(1)} copy(f32[64,256,3]{2,1,0:T(8,128)} %bitcast.120) | data formatting | bytes 393216 | tf_op jit(solution)/shard_map/gather | solution.py:37
  144.3 5.4 %all_gather.17 = f32[16384]{0:T(1024)S(1)} all-gather(f32[4096]{0:T(1024)S(1)} %copy-done.6), channel_id=1, replica_groups=mesh['dom'=8,'sub'=4] {'sub'}, dimensions={0}, use_global_device_ids=true | all-gather | bytes 81920 | tf_op jit(solution)/shard_map/all_gather | solution.py:102
  149.8 90.5 %gather_fusion.5 = f32[16384]{0:T(1024)S(1)} fusion(f32[16384]{0:T(1024)S(1)} %all_gather.17, s32[16384]{0:T(1024)S(1)} %broadcast_clamp_fusion), kind=kCustom, calls=%fused_computation.5 | custom fusion | bytes 196608 | tf_op jit(solution)/shard_map/gather | solution.py:38
  240.6 160.7 %while.36 = (s32[]{:T(128)}, f32[16,8,3,256]{3,2,1,0:T(4,128)}, f32[16,8,3,256]{3,1,0,2:T(8,128)S(1)}, s32[16,8]{1,0:T(8,128)S(1)}, f32[64,3,256]{2,1,0:T(4,128)...) while((s32[]{:T(128)}, f32[16,8,3,256]{3,2,1,0:T(4,128)}, ...), condition=%wide.region_20.21_spmd, body=%wide.region_17.20_spmd.sunk | while | flops 45615144 | bytes 8758177 | solution.py:53
  241.3 1.1 fusion.88
  243.1 5.9 %fusion.90 = f32[8,256,256]{2,1,0:T(8,128)S(1)} fusion(f32[8,256,256]{2,1,0:T(8,128)S(1)} %fusion.88, f32[8,256]{1,0:T(8,128)S(1)} %broadcast_multiply_fusion.3), kind=kLoop, calls=%fused_computation.57.clone.1 | loop fusion | flops 36700160 | bytes 4202496 | tf_op jit(solution)/shard_map/while/body/eval_jaxpr/vmap()/div | solution.py:31
  251.4 1.1 fusion.88
  253.1 5.9 %fusion.90 = f32[8,256,256]{2,1,0:T(8,128)S(1)} fusion(f32[8,256,256]{2,1,0:T(8,128)S(1)} %fusion.88, f32[8,256]{1,0:T(8,128)S(1)} %broadcast_multiply_fusion.3), kind=kLoop, calls=%fused_computation.57.clone.1 | loop fusion | flops 36700160 | bytes 4202496 | tf_op jit(solution)/shard_map/while/body/eval_jaxpr/vmap()/div | solution.py:31
  261.4 1.1 fusion.88
  263.2 5.9 %fusion.90 = f32[8,256,256]{2,1,0:T(8,128)S(1)} fusion(f32[8,256,256]{2,1,0:T(8,128)S(1)} %fusion.88, f32[8,256]{1,0:T(8,128)S(1)} %broadcast_multiply_fusion.3), kind=kLoop, calls=%fused_computation.57.clone.1 | loop fusion | flops 36700160 | bytes 4202496 | tf_op jit(solution)/shard_map/while/body/eval_jaxpr/vmap()/div | solution.py:31
  271.4 1.1 fusion.88
  273.2 5.9 %fusion.90 = f32[8,256,256]{2,1,0:T(8,128)S(1)} fusion(f32[8,256,256]{2,1,0:T(8,128)S(1)} %fusion.88, f32[8,256]{1,0:T(8,128)S(1)} %broadcast_multiply_fusion.3), kind=kLoop, calls=%fused_computation.57.clone.1 | loop fusion | flops 36700160 | bytes 4202496 | tf_op jit(solution)/shard_map/while/body/eval_jaxpr/vmap()/div | solution.py:31
  281.5 1.1 fusion.88
  283.3 5.9 %fusion.90 = f32[8,256,256]{2,1,0:T(8,128)S(1)} fusion(f32[8,256,256]{2,1,0:T(8,128)S(1)} %fusion.88, f32[8,256]{1,0:T(8,128)S(1)} %broadcast_multiply_fusion.3), kind=kLoop, calls=%fused_computation.57.clone.1 | loop fusion | flops 36700160 | bytes 4202496 | tf_op jit(solution)/shard_map/while/body/eval_jaxpr/vmap()/div | solution.py:31
  291.5 1.1 fusion.88
  293.3 5.9 %fusion.90 = f32[8,256,256]{2,1,0:T(8,128)S(1)} fusion(f32[8,256,256]{2,1,0:T(8,128)S(1)} %fusion.88, f32[8,256]{1,0:T(8,128)S(1)} %broadcast_multiply_fusion.3), kind=kLoop, calls=%fused_computation.57.clone.1 | loop fusion | flops 36700160 | bytes 4202496 | tf_op jit(solution)/shard_map/while/body/eval_jaxpr/vmap()/div | solution.py:31
  301.6 1.1 fusion.88
  303.4 5.9 %fusion.90 = f32[8,256,256]{2,1,0:T(8,128)S(1)} fusion(f32[8,256,256]{2,1,0:T(8,128)S(1)} %fusion.88, f32[8,256]{1,0:T(8,128)S(1)} %broadcast_multiply_fusion.3), kind=kLoop, calls=%fused_computation.57.clone.1 | loop fusion | flops 36700160 | bytes 4202496 | tf_op jit(solution)/shard_map/while/body/eval_jaxpr/vmap()/div | solution.py:31
  313.4 5.9 %fusion.90 = f32[8,256,256]{2,1,0:T(8,128)S(1)} fusion(f32[8,256,256]{2,1,0:T(8,128)S(1)} %fusion.88, f32[8,256]{1,0:T(8,128)S(1)} %broadcast_multiply_fusion.3), kind=kLoop, calls=%fused_computation.57.clone.1 | loop fusion | flops 36700160 | bytes 4202496 | tf_op jit(solution)/shard_map/while/body/eval_jaxpr/vmap()/div | solution.py:31
  323.4 5.9 %fusion.90 = f32[8,256,256]{2,1,0:T(8,128)S(1)} fusion(f32[8,256,256]{2,1,0:T(8,128)S(1)} %fusion.88, f32[8,256]{1,0:T(8,128)S(1)} %broadcast_multiply_fusion.3), kind=kLoop, calls=%fused_computation.57.clone.1 | loop fusion | flops 36700160 | bytes 4202496 | tf_op jit(solution)/shard_map/while/body/eval_jaxpr/vmap()/div | solution.py:31
  331.7 1.1 fusion.88
  333.5 5.9 %fusion.90 = f32[8,256,256]{2,1,0:T(8,128)S(1)} fusion(f32[8,256,256]{2,1,0:T(8,128)S(1)} %fusion.88, f32[8,256]{1,0:T(8,128)S(1)} %broadcast_multiply_fusion.3), kind=kLoop, calls=%fused_computation.57.clone.1 | loop fusion | flops 36700160 | bytes 4202496 | tf_op jit(solution)/shard_map/while/body/eval_jaxpr/vmap()/div | solution.py:31
  343.5 5.9 %fusion.90 = f32[8,256,256]{2,1,0:T(8,128)S(1)} fusion(f32[8,256,256]{2,1,0:T(8,128)S(1)} %fusion.88, f32[8,256]{1,0:T(8,128)S(1)} %broadcast_multiply_fusion.3), kind=kLoop, calls=%fused_computation.57.clone.1 | loop fusion | flops 36700160 | bytes 4202496 | tf_op jit(solution)/shard_map/while/body/eval_jaxpr/vmap()/div | solution.py:31
  353.6 5.9 %fusion.90 = f32[8,256,256]{2,1,0:T(8,128)S(1)} fusion(f32[8,256,256]{2,1,0:T(8,128)S(1)} %fusion.88, f32[8,256]{1,0:T(8,128)S(1)} %broadcast_multiply_fusion.3), kind=kLoop, calls=%fused_computation.57.clone.1 | loop fusion | flops 36700160 | bytes 4202496 | tf_op jit(solution)/shard_map/while/body/eval_jaxpr/vmap()/div | solution.py:31
  361.8 1.1 fusion.88
  363.6 5.9 %fusion.90 = f32[8,256,256]{2,1,0:T(8,128)S(1)} fusion(f32[8,256,256]{2,1,0:T(8,128)S(1)} %fusion.88, f32[8,256]{1,0:T(8,128)S(1)} %broadcast_multiply_fusion.3), kind=kLoop, calls=%fused_computation.57.clone.1 | loop fusion | flops 36700160 | bytes 4202496 | tf_op jit(solution)/shard_map/while/body/eval_jaxpr/vmap()/div | solution.py:31
  373.7 5.9 %fusion.90 = f32[8,256,256]{2,1,0:T(8,128)S(1)} fusion(f32[8,256,256]{2,1,0:T(8,128)S(1)} %fusion.88, f32[8,256]{1,0:T(8,128)S(1)} %broadcast_multiply_fusion.3), kind=kLoop, calls=%fused_computation.57.clone.1 | loop fusion | flops 36700160 | bytes 4202496 | tf_op jit(solution)/shard_map/while/body/eval_jaxpr/vmap()/div | solution.py:31
  381.9 1.1 fusion.88
  383.7 5.9 %fusion.90 = f32[8,256,256]{2,1,0:T(8,128)S(1)} fusion(f32[8,256,256]{2,1,0:T(8,128)S(1)} %fusion.88, f32[8,256]{1,0:T(8,128)S(1)} %broadcast_multiply_fusion.3), kind=kLoop, calls=%fused_computation.57.clone.1 | loop fusion | flops 36700160 | bytes 4202496 | tf_op jit(solution)/shard_map/while/body/eval_jaxpr/vmap()/div | solution.py:31
  393.7 5.9 %fusion.90 = f32[8,256,256]{2,1,0:T(8,128)S(1)} fusion(f32[8,256,256]{2,1,0:T(8,128)S(1)} %fusion.88, f32[8,256]{1,0:T(8,128)S(1)} %broadcast_multiply_fusion.3), kind=kLoop, calls=%fused_computation.57.clone.1 | loop fusion | flops 36700160 | bytes 4202496 | tf_op jit(solution)/shard_map/while/body/eval_jaxpr/vmap()/div | solution.py:31
  401.3 1.9 copy.114
  403.2 5.9 %all-to-all-start.5 = ((f32[8,16,3,256]{3,1,2,0:T(8,128)}), f32[8,16,3,256]{3,1,2,0:T(8,128)S(1)}, u32[]{:S(2)}, u32[]{:S(2)}) async-start(f32[8,16,3,256]{3,1,2,0:T(8,128)} %copy.114), calls=%async_computation.5 | async-start | bytes 786432 | tf_op jit(solution)/shard_map/all_to_all | solution.py:163
  409.6 11.7 %all-to-all-done.5 = f32[8,16,3,256]{3,1,2,0:T(8,128)S(1)} async-done(((f32[8,16,3,256]{3,1,2,0:T(8,128)}), f32[8,16,3,256]{3,1,2,0:T(8,128)S(1)}, u32[]{:S(2)}, u32[]{:S(2)}) %all-to-all-start.5) | async-done | bytes 393248 | tf_op jit(solution)/shard_map/all_to_all | solution.py:163
  421.6 1.3 gather_fusion.12
  424.1 3.5 all-to-all-start.6
  427.6 80.5 %while.34 = (s32[]{:T(128)}, f32[8,8,3,256]{3,2,1,0:T(4,128)}, f32[8,8,3,256]{3,2,1,0:T(4,128)S(1)}, s32[8,8]{1,0:T(8,128)S(1)}, f32[64,3,256]{2,1,0:T(4,128)S(1)}, /*index=5*/f32[64,256]{1,0:T(8,128)S(1)}, s32[]{:T(128)}) while((s32[]{:T(128)}, f32[8,8,3,256]{3,2,1,0:T(4,128)}, f32[8,8,3,256]{3,2,1,0:T(4,128)S(1)}, s32[8,8]{1,0:T(8,128)S(1)}, ...), condition=%wide.region_3.4_spmd, body=%wide.region_0.3_spmd.sunk | while | flops 45613096 | bytes 10265453 | solution.py:53
  430.1 5.9 %fusion.86 = f32[8,256,256]{2,1,0:T(8,128)S(1)} fusion(f32[8,256,256]{2,1,0:T(8,128)S(1)} %fusion.85, f32[8,256]{1,0:T(8,128)S(1)} %gather_fusion.1), kind=kLoop, calls=%fused_computation.27.clone.1 | loop fusion | flops 36700160 | bytes 4202496 | tf_op jit(solution)/shard_map/while/body/eval_jaxpr/vmap()/div | solution.py:31
  440.1 5.9 %fusion.86 = f32[8,256,256]{2,1,0:T(8,128)S(1)} fusion(f32[8,256,256]{2,1,0:T(8,128)S(1)} %fusion.85, f32[8,256]{1,0:T(8,128)S(1)} %gather_fusion.1), kind=kLoop, calls=%fused_computation.27.clone.1 | loop fusion | flops 36700160 | bytes 4202496 | tf_op jit(solution)/shard_map/while/body/eval_jaxpr/vmap()/div | solution.py:31
  450.2 5.9 %fusion.86 = f32[8,256,256]{2,1,0:T(8,128)S(1)} fusion(f32[8,256,256]{2,1,0:T(8,128)S(1)} %fusion.85, f32[8,256]{1,0:T(8,128)S(1)} %gather_fusion.1), kind=kLoop, calls=%fused_computation.27.clone.1 | loop fusion | flops 36700160 | bytes 4202496 | tf_op jit(solution)/shard_map/while/body/eval_jaxpr/vmap()/div | solution.py:31
  460.2 5.9 %fusion.86 = f32[8,256,256]{2,1,0:T(8,128)S(1)} fusion(f32[8,256,256]{2,1,0:T(8,128)S(1)} %fusion.85, f32[8,256]{1,0:T(8,128)S(1)} %gather_fusion.1), kind=kLoop, calls=%fused_computation.27.clone.1 | loop fusion | flops 36700160 | bytes 4202496 | tf_op jit(solution)/shard_map/while/body/eval_jaxpr/vmap()/div | solution.py:31
  470.3 5.9 %fusion.86 = f32[8,256,256]{2,1,0:T(8,128)S(1)} fusion(f32[8,256,256]{2,1,0:T(8,128)S(1)} %fusion.85, f32[8,256]{1,0:T(8,128)S(1)} %gather_fusion.1), kind=kLoop, calls=%fused_computation.27.clone.1 | loop fusion | flops 36700160 | bytes 4202496 | tf_op jit(solution)/shard_map/while/body/eval_jaxpr/vmap()/div | solution.py:31
  480.3 5.9 %fusion.86 = f32[8,256,256]{2,1,0:T(8,128)S(1)} fusion(f32[8,256,256]{2,1,0:T(8,128)S(1)} %fusion.85, f32[8,256]{1,0:T(8,128)S(1)} %gather_fusion.1), kind=kLoop, calls=%fused_computation.27.clone.1 | loop fusion | flops 36700160 | bytes 4202496 | tf_op jit(solution)/shard_map/while/body/eval_jaxpr/vmap()/div | solution.py:31
  490.4 5.9 %fusion.86 = f32[8,256,256]{2,1,0:T(8,128)S(1)} fusion(f32[8,256,256]{2,1,0:T(8,128)S(1)} %fusion.85, f32[8,256]{1,0:T(8,128)S(1)} %gather_fusion.1), kind=kLoop, calls=%fused_computation.27.clone.1 | loop fusion | flops 36700160 | bytes 4202496 | tf_op jit(solution)/shard_map/while/body/eval_jaxpr/vmap()/div | solution.py:31
  500.5 5.9 %fusion.86 = f32[8,256,256]{2,1,0:T(8,128)S(1)} fusion(f32[8,256,256]{2,1,0:T(8,128)S(1)} %fusion.85, f32[8,256]{1,0:T(8,128)S(1)} %gather_fusion.1), kind=kLoop, calls=%fused_computation.27.clone.1 | loop fusion | flops 36700160 | bytes 4202496 | tf_op jit(solution)/shard_map/while/body/eval_jaxpr/vmap()/div | solution.py:31
  509.1 1.3 gather_fusion.13
  (347 shorter events, 104.6 us)
Async XLA Ops:
  0.0 29.6 %copy-start = (f32[64,3,256]{2,0,1:T(8,128)S(1)}, f32[64,3,256]{2,0,1:T(8,128)}, u32[]{:S(2)}) copy-start(f32[64,3,256]{2,0,1:T(8,128)} %param.15) | copy-start | bytes 589828
  24.4 8.3 %all-to-all-start = ((s32[4,8,8]{2,1,0:T(8,128)}), s32[4,8,8]{2,1,0:T(8,128)S(1)}, u32[]{:S(2)}, u32[]{:S(2)}) async-start(s32[4,8,8]{2,1,0:T(8,128)} %get-tuple-element.261), calls=%async_computation | async-start | bytes 32768 | tf_op jit(solution)/shard_map/all_to_all | solution.py:136
  29.6 3.0 copy-start.4
  32.7 7.1 %all-to-all-start.1 = ((s32[4,8,8]{2,1,0:T(8,128)}), s32[4,8,8]{2,1,0:T(8,128)S(1)}, u32[]{:S(2)}, u32[]{:S(2)}) async-start(s32[4,8,8]{2,1,0:T(8,128)} %get-tuple-element.260), calls=%async_computation.1 | async-start | bytes 32768 | tf_op jit(solution)/shard_map/all_to_all | solution.py:135
  39.8 15.1 %all-to-all-start.2 = ((f32[4,8,8,3,256]{4,2,1,3,0:T(8,128)}), f32[4,8,8,3,256]{4,2,1,3,0:T(8,128)S(1)}, u32[]{:S(2)}, u32[]{:S(2)}) async-start(f32[4,8,8,3,256]{4,2,1,3,0:T(8,128)} %copy_select_fusion), calls=%async_computation.2 | async-start | bytes 1572864 | tf_op jit(solution)/shard_map/all_to_all | solution.py:134
  54.9 12.3 %all-to-all-start.4 = ((s32[8,1,16]{2,1,0:T(1,128)}), s32[8,1,16]{2,1,0:T(1,128)S(1)}, u32[]{:S(2)}, u32[]{:S(2)}) async-start(s32[8,1,16]{2,1,0:T(1,128)} %bitcast.40), calls=%async_computation.4 | async-start | bytes 8192 | tf_op jit(solution)/shard_map/all_to_all | solution.py:152
  60.7 9.9 %copy-start.3 = (f32[3,4096]{1,0:T(4,128)S(1)}, f32[3,4096]{1,0:T(4,128)}, u32[]{:S(2)}) copy-start(f32[3,4096]{1,0:T(4,128)} %param.20) | copy-start | bytes 147460
  67.1 173.5 %all-to-all-start.3 = ((f32[8,16,3,256]{3,1,2,0:T(8,128)}), f32[8,16,3,256]{3,1,2,0:T(8,128)S(1)}, u32[]{:S(2)}, u32[]{:S(2)}) async-start(f32[8,16,3,256]{3,1,2,0:T(8,128)} %copy_select_fusion.1), calls=%async_computation.3 | async-start | bytes 786432 | tf_op jit(solution)/shard_map/all_to_all | solution.py:151
  139.0 5.4 %copy-start.6 = (f32[4096]{0:T(1024)S(1)}, f32[4096]{0:T(1024)}, u32[]{:S(2)}) copy-start(f32[4096]{0:T(1024)} %param.21) | copy-start | bytes 49156
  149.8 90.6 %copy-start.7 = (s32[64]{0:T(128)S(1)}, s32[64]{0:T(128)}, u32[]{:S(2)}) copy-start(s32[64]{0:T(128)} %param.23) | copy-start | bytes 772
  401.3 7.9 %copy-start.8 = (s32[64]{0:T(128)S(1)}, s32[64]{0:T(128)}, u32[]{:S(2)}) copy-start(s32[64]{0:T(128)} %param.17) | copy-start | bytes 772
  403.2 18.1 %all-to-all-start.5 = ((f32[8,16,3,256]{3,1,2,0:T(8,128)}), f32[8,16,3,256]{3,1,2,0:T(8,128)S(1)}, u32[]{:S(2)}, u32[]{:S(2)}) async-start(f32[8,16,3,256]{3,1,2,0:T(8,128)} %copy.114), calls=%async_computation.5 | async-start | bytes 786432 | tf_op jit(solution)/shard_map/all_to_all | solution.py:163
  424.1 84.4 %all-to-all-start.6 = ((f32[4,8,8,3,256]{4,2,3,1,0:T(8,128)}), f32[4,8,8,3,256]{4,2,3,1,0:T(8,128)S(1)}, u32[]{:S(2)}, u32[]{:S(2)}) async-start(f32[4,8,8,3,256]{4,2,3,1,0:T(8,128)} %copy.118), calls=%async_computation.6 | async-start | bytes 1572864 | tf_op jit(solution)/shard_map/all_to_all | solution.py:168
  427.6 80.8 %copy-start.5 = (s32[64,256]{1,0:T(8,128)S(1)}, s32[64,256]{1,0:T(8,128)}, u32[]{:S(2)}) copy-start(s32[64,256]{1,0:T(8,128)} %param.16) | copy-start | bytes 196612
  427.6 0.7 copy-start.1
  436.0 1.7 copy-start.2
  437.7 0.7 copy-start.1
  446.0 1.7 copy-start.2
  447.7 0.7 copy-start.1
  456.1 1.7 copy-start.2
  457.8 0.7 copy-start.1
  466.1 1.7 copy-start.2
  467.9 0.7 copy-start.1
  476.2 1.7 copy-start.2
  477.9 0.7 copy-start.1
  486.2 1.7 copy-start.2
  488.0 0.7 copy-start.1
  496.3 1.7 copy-start.2
  498.0 0.7 copy-start.1
  506.4 1.7 copy-start.2
